TPU v7x, 256 devices: a whole 4x4x8 slice. The times are simulated.
256 devices in a mesh: ma: 64 (over x, z, core), freq: 4 (over y).
Axes of the slice: x: 4, y: 4, z: 8, core: 2. Of those that a mesh axis runs over, the one named last changes fastest.
Arguments:
- visibilities: bfloat16 [128, 192, 16, 2, 512], P('ma', None, 'freq')
- eigenmodes: bfloat16 [128, 16, 2, 512, 256], P('ma', 'freq'), may hold values from -0.375 to 0.375
- retained: int32 [128], P('ma'), may hold values from 1 to 256
Outputs:
- coefficients: bfloat16 [128, 2, 192, 256], P('ma')
- filtered: bfloat16 [128, 192, 16, 2, 512], P('ma', None, 'freq')
All inputs are finite; a program needn't handle non-finite values.
Results may differ from a plain program's by a relative error of at most 0.0049.
Values may be sent and summed in bfloat16 or wider, within the bound.
A program may use at most 128 MiB of HBM per device.

v0:
```python
import jax
import jax.numpy as jnp
from jax import lax
from jax.sharding import PartitionSpec as P


def in_blocks(x, dim, count):
    before, after = (x.shape[:dim], x.shape[dim + 1 :])
    return jnp.moveaxis(x.reshape(*before, count, -1, *after), dim, 0)


def summed_on_arrival(x, axis, dim):
    pieces = in_blocks(x, dim, lax.axis_size(axis))
    arrived = lax.all_to_all(pieces, axis, split_axis=0, concat_axis=0, tiled=True)
    return arrived.sum(axis=0)


def sent_together(arrays, axis, dim, along):
    ends, at = ([], 0)
    for a in arrays[:-1]:
        at += a.shape[along]
        ends.append(at)
    both = jnp.concatenate(arrays, axis=along)
    return tuple(jnp.split(summed_on_arrival(both, axis, dim), ends, axis=along))


def copy_for_each(x, axis):
    count = lax.axis_size(axis)
    return lax.all_to_all(jnp.broadcast_to(x[None], (count, *x.shape)), axis, 0, 0, tiled=True)


def of_everyone(x, axis):
    return copy_for_each(x, axis).sum(axis=0)


def together(arrays, axis):
    ends = [0]
    for a in arrays:
        ends.append(ends[-1] + a.size)
    running = of_everyone(jnp.concatenate([a.ravel() for a in arrays]), axis)
    return tuple((running[b:e].reshape(a.shape) for a, b, e in zip(arrays, ends, ends[1:])))


def gather_turned(arrays, axis, dims):
    turned = [jnp.moveaxis(a, dim, 0) for a, dim in zip(arrays, dims)]
    widths = [t[0].size for t in turned]
    both = jnp.concatenate([t.reshape(-1, w) for t, w in zip(turned, widths)], axis=1)
    filled = lax.all_gather(both, axis, axis=0, tiled=True)
    pieces = jnp.split(filled, [sum(widths[:k]) for k in range(1, len(widths))], axis=1)
    return tuple(
        (
            jnp.moveaxis(b.reshape(-1, *t.shape[1:]), 0, dim)
            for b, t, dim in zip(pieces, turned, dims)
        )
    )


def per_device(visibilities, eigenmodes, retained):
    local_modes, samples, local_freqs, _, base = visibilities.shape
    kmax = eigenmodes.shape[-1]
    width = local_freqs * 2 * base
    flat = visibilities.reshape(local_modes, samples, width)
    swapped = jnp.stack(
        [visibilities[:, :, :, 1, :], -visibilities[:, :, :, 0, :]], axis=3
    ).reshape(local_modes, samples, width)
    matrix = eigenmodes.reshape(local_modes, width, kmax)
    part_re = jnp.einsum("msc,mck->msk", flat, matrix, preferred_element_type=jnp.float32)
    part_im = jnp.einsum("msc,mck->msk", swapped, matrix, preferred_element_type=jnp.float32)
    share_re, share_im = sent_together((part_re, part_im), "freq", 2, 0)
    first_col = lax.axis_index("freq") * share_re.shape[2]
    columns = share_re.shape[2]
    ranks = first_col + jnp.arange(columns, dtype=jnp.int32)
    keep = (ranks[None, :] < retained[:, None]).astype(jnp.float32)
    power = jnp.sum(keep[:, None, :] * (share_re * share_re + share_im * share_im), axis=(0, 1))
    count = jnp.float32(samples) * jnp.sum(keep, axis=0)
    keep, power, count = (keep, power, count)
    power, count = together((power, count), "ma")
    scale = 1.0 / jnp.sqrt(power / jnp.maximum(count, 1.0) + 1e-06)
    gain = keep * scale[None, :]
    piece_re = (share_re * gain[:, None, :]).astype(jnp.bfloat16)
    piece_im = (share_im * gain[:, None, :]).astype(jnp.bfloat16)
    coef_re, coef_im = gather_turned((piece_re, piece_im), "freq", (2, 2))
    first = jnp.einsum("msk,mck->msc", coef_re, matrix, preferred_element_type=jnp.float32).reshape(
        local_modes, samples, local_freqs, 2, base
    )
    second = jnp.einsum(
        "msk,mck->msc", coef_im, matrix, preferred_element_type=jnp.float32
    ).reshape(local_modes, samples, local_freqs, 2, base)
    out_re = first[:, :, :, 0, :] - second[:, :, :, 1, :]
    out_im = second[:, :, :, 0, :] + first[:, :, :, 1, :]
    filtered = jnp.stack([out_re, out_im], axis=3).astype(jnp.bfloat16)
    coefficients = jnp.stack([coef_re, coef_im], axis=1)
    return (coefficients, filtered)


def solution(mesh):
    return jax.shard_map(
        per_device,
        mesh=mesh,
        in_specs=(P("ma", None, "freq", None, None), P("ma", "freq", None, None, None), P("ma")),
        out_specs=(P("ma", None, None, None), P("ma", None, "freq", None, None)),
        check_vma=False,
    )
```

profile of v0, /device:TPU:1, one launch (start us, length us, event | category | flops | bytes accessed | tf_op | source)
XLA Modules:
  0.0 145.2 jit_solution(11882476951754866582)
XLA Ops:
  0.6 6.3 %reshape.100 = bf16[2,192,4096]{2,1,0:T(8,128)(2,1)} reshape(bf16[2,192,4,2,512]{4,3,2,1,0:T(2,128)(2,1)} %param.3) | data formatting | bytes 6291456 | tf_op jit(solution)/shard_map/reshape | solution.py:62
  6.9 5.8 %fusion.5 = (bf16[2,192,4,1,512]{4,3,2,1,0:T(2,128)(2,1)S(1)}, bf16[2,192,4,1,512]{4,3,2,1,0:T(2,128)(2,1)S(1)}) fusion(bf16[2,192,4,2,512]{4,3,2,1,0:T(2,128)(2,1)S(1)} %copy-done.1), kind=kLoop, calls=%fused_computation.23 | loop fusion | flops 786432 | bytes 6291456 | tf_op jit(solution)/shard_map/slice | solution.py:64
  12.7 8.0 %pad_maximum_fusion = bf16[2,192,4,2,512]{4,3,2,1,0:T(2,128)(2,1)} fusion(bf16[2,192,4,1,512]{4,3,2,1,0:T(2,128)(2,1)S(1)} %get-tuple-element.17, bf16[2,192,4,1,512]{4,3,2,1,0:T(2,128)(2,1)S(1)} %get-tuple-element.16), kind=kLoop, calls=%fused_computation.4 | loop fusion | flops 6291456 | bytes 6291456 | tf_op jit(solution)/shard_map/stack | solution.py:63
  20.7 6.3 %reshape.102 = bf16[2,192,4096]{2,1,0:T(8,128)(2,1)} reshape(bf16[2,192,4,2,512]{4,3,2,1,0:T(2,128)(2,1)} %pad_maximum_fusion) | data formatting | bytes 6291456 | tf_op jit(solution)/shard_map/reshape | solution.py:65
  27.0 3.3 %fusion.7 = f32[2,192,256]{2,1,0:T(8,128)S(1)} fusion(bf16[2,192,4096]{2,1,0:T(8,128)(2,1)S(1)} %copy-done.2, bf16[2,4096,256]{2,1,0:T(8,128)(2,1)} %bitcast.27), kind=kOutput, calls=%fused_computation.25 | convolution fusion | flops 805306368 | bytes 7733248 | tf_op jit(solution)/shard_map/msc,mck->msk/dot_general | solution.py:67
  30.4 0.1 copy-done
  30.5 1.0 copy-done.3
  31.5 1.0 fusion.8
  32.5 0.3 copy.30
  32.8 1.1 copy.31
  33.9 5.0 %all-to-all-start = ((f32[4,4,192,64]{2,3,1,0:T(8,128)}), f32[4,4,192,64]{2,3,1,0:T(8,128)S(1)}, u32[]{:S(2)}, u32[]{:S(2)}) async-start(f32[4,4,192,64]{2,3,1,0:T(8,128)} %copy.31), calls=%async_computation | async-start | bytes 2097152 | tf_op jit(solution)/shard_map/all_to_all | solution.py:14
  39.1 13.3 %all-to-all-done = f32[4,4,192,64]{2,3,1,0:T(8,128)S(1)} async-done(((f32[4,4,192,64]{2,3,1,0:T(8,128)}), f32[4,4,192,64]{2,3,1,0:T(8,128)S(1)}, u32[]{:S(2)}, u32[]{:S(2)}) %all-to-all-start) | async-done | bytes 786464 | tf_op jit(solution)/shard_map/all_to_all | solution.py:14
  52.5 0.2 multiply_reduce_fusion
  52.8 23.1 %all_to_all.11 = f32[64,1,128]{2,1,0:T(1,128)S(1)} all-to-all(f32[64,1,128]{2,1,0:T(1,128)S(1)} %broadcast_in_dim.2), channel_id=1, replica_groups=mesh['ma'=64,'freq'=4] {'ma'}, dimensions={0} | all-to-all | bytes 65536 | tf_op jit(solution)/shard_map/all_to_all | solution.py:29
  76.6 9.8 %all_gather.3 = bf16[256,768]{1,0:T(8,128)(2,1)S(1)} all-gather(bf16[64,768]{1,0:T(8,128)(2,1)S(1)} %pad_maximum_fusion.4), channel_id=1, replica_groups=mesh['ma'=64,'freq'=4] {'freq'}, dimensions={0}, use_global_device_ids=true | all-gather | bytes 491520 | tf_op jit(solution)/shard_map/all_gather | solution.py:48
  86.5 0.1 copy.36
  86.6 0.1 copy.37
  86.8 0.8 copy.38
  87.6 6.4 %fusion.10 = f32[2,192,4096]{2,1,0:T(8,128)} fusion(bf16[2,192,256]{2,1,0:T(8,128)(2,1)S(1)} %bitcast.35, bf16[2,4096,256]{2,1,0:T(8,128)(2,1)} %bitcast.28), kind=kOutput, calls=%fused_computation.28 | convolution fusion | flops 805306368 | bytes 10682368 | tf_op jit(solution)/shard_map/msk,mck->msc/dot_general | solution.py:86
  94.0 9.2 %reshape.109 = f32[2,192,4,2,512]{4,3,2,1,0:T(2,128)} reshape(f32[2,192,4096]{2,1,0:T(8,128)} %fusion.10) | data formatting | bytes 12582912 | tf_op jit(solution)/shard_map/reshape | solution.py:88
  103.1 6.3 %fusion.9 = f32[2,192,4096]{2,1,0:T(8,128)} fusion(bf16[2,192,256]{2,1,0:T(8,128)(2,1)S(1)} %bitcast.33, bf16[2,4096,256]{2,1,0:T(8,128)(2,1)} %bitcast.29), kind=kOutput, calls=%fused_computation.27 | convolution fusion | flops 805306368 | bytes 10682368 | tf_op jit(solution)/shard_map/msk,mck->msc/dot_general | solution.py:83
  109.5 9.1 %reshape.108 = f32[2,192,4,2,512]{4,3,2,1,0:T(2,128)} reshape(f32[2,192,4096]{2,1,0:T(8,128)} %fusion.9) | data formatting | bytes 12582912 | tf_op jit(solution)/shard_map/reshape | solution.py:83
  118.6 18.5 %fusion.1 = (bf16[2,192,4,1,512]{4,3,2,1,0:T(2,128)(2,1)S(1)}, bf16[2,192,4,1,512]{4,3,2,1,0:T(2,128)(2,1)S(1)}) fusion(f32[2,192,4,2,512]{4,3,2,1,0:T(2,128)} %reshape.109, f32[2,192,4,2,512]{4,3,2,1,0:T(2,128)} %reshape.108), kind=kLoop, calls=%fused_computation.3 | loop fusion | flops 3145728 | bytes 15728640 | tf_op jit(solution)/shard_map/convert
  137.2 8.0 %pad_maximum_fusion.1 = bf16[2,192,4,2,512]{4,3,2,1,0:T(2,128)(2,1)} fusion(bf16[2,192,4,1,512]{4,3,2,1,0:T(2,128)(2,1)S(1)} %get-tuple-element.15, bf16[2,192,4,1,512]{4,3,2,1,0:T(2,128)(2,1)S(1)} %get-tuple-element.14), kind=kLoop, calls=%fused_computation.5 | loop fusion | flops 6291456 | bytes 6291456 | tf_op jit(solution)/shard_map/stack | solution.py:91
  (27 shorter events, 1.1 us)
Async XLA Ops:
  0.6 6.3 %copy-start.1 = (bf16[2,192,4,2,512]{4,3,2,1,0:T(2,128)(2,1)S(1)}, bf16[2,192,4,2,512]{4,3,2,1,0:T(2,128)(2,1)}, u32[]{:S(2)}) copy-start(bf16[2,192,4,2,512]{4,3,2,1,0:T(2,128)(2,1)} %param.3) | copy-start | bytes 9437188
  20.7 6.3 %copy-start.2 = (bf16[2,192,4096]{2,1,0:T(8,128)(2,1)S(1)}, bf16[2,192,4096]{2,1,0:T(8,128)(2,1)}, u32[]{:S(2)}) copy-start(bf16[2,192,4096]{2,1,0:T(8,128)(2,1)} %reshape.100) | copy-start | bytes 9437188
  27.0 3.4 %copy-start = (bf16[2,4,2,512,256]{4,3,2,1,0:T(8,128)(2,1)S(1)}, bf16[2,4,2,512,256]{4,3,2,1,0:T(8,128)(2,1)}, u32[]{:S(2)}) copy-start(bf16[2,4,2,512,256]{4,3,2,1,0:T(8,128)(2,1)} %param.4) | copy-start | bytes 12582916
  27.0 4.4 %copy-start.3 = (bf16[2,192,4096]{2,1,0:T(8,128)(2,1)S(1)}, bf16[2,192,4096]{2,1,0:T(8,128)(2,1)}, u32[]{:S(2)}) copy-start(bf16[2,192,4096]{2,1,0:T(8,128)(2,1)} %reshape.102) | copy-start | bytes 9437188
  32.5 6.4 %copy-start.4 = (s32[2]{0:T(128)S(1)}, s32[2]{0:T(128)}, u32[]{:S(2)}) copy-start(s32[2]{0:T(128)} %param.5) | copy-start | bytes 28
  33.9 18.5 %all-to-all-start = ((f32[4,4,192,64]{2,3,1,0:T(8,128)}), f32[4,4,192,64]{2,3,1,0:T(8,128)S(1)}, u32[]{:S(2)}, u32[]{:S(2)}) async-start(f32[4,4,192,64]{2,3,1,0:T(8,128)} %copy.31), calls=%async_computation | async-start | bytes 2097152 | tf_op jit(solution)/shard_map/all_to_all | solution.py:14
where the time goes:
time: 148 us; the launch traced here: 145 us
  other arithmetic  41.3 us (28%)
  local copies, waits for them, and re-layouts  34.9 us (24%)
  blocking collectives  33 us (22%)
  matrix products  17 us (11%)
  waiting for transfers between devices  13.3 us (9%)
  starting transfers between devices  5 us (3%)
    all_to_all x1, blocking collectives, copy_for_each(): lax.all_to_all(jnp.broadcast_to(x[None], (count, *x.shape)), axis, 0, 0,...  23.1 us
    another operation x1, other arithmetic  18.5 us
    all_to_all x1, waiting for transfers between devices, summed_on_arrival(): lax.all_to_all(pieces, axis, split_axis=0, concat_axis=0, tiled=True)  13.3 us
    all_gather x1, blocking collectives, gather_turned(): filled = lax.all_gather(both, axis, axis=0, tiled=True)  9.82 us
    reshape x1, local copies, waits for them, and re-layouts, per_device(): second = jnp.einsum('msk,mck->msc', coef_im, matrix, preferred_element_ty...  9.18 us
    reshape x1, local copies, waits for them, and re-layouts, per_device(): jnp.einsum('msk,mck->msc', coef_re, matrix, preferred_element_type=jnp.fl...  9.15 us
    another operation x1, other arithmetic, per_device(): filtered = jnp.stack([out_re, out_im], axis=3).astype(jnp.bfloat16)  8.05 us
    another operation x1, other arithmetic, per_device(): jnp.stack([visibilities[:, :, :, 1, :], -visibilities[:, :, :, 0, :]], ax...  8.05 us
  transfers between devices with their start and end apart: 1, of which 1 were waited for; matrix products, arithmetic and copies ran while one was open for 0% of the time, Pallas kernels for 0%

commit v1 on v0

v1 whole, which is shorter than its diff:
```python
import functools

import jax
import jax.numpy as jnp
from jax import lax
from jax.experimental import pallas as pl
from jax.experimental.pallas import tpu as pltpu
from jax.sharding import PartitionSpec as P

MESH = pl.DeviceIdType.MESH
BF16, F32 = jnp.bfloat16, jnp.float32
NX, NZ, NCORE, NY = 4, 8, 2, 4
LANES = 128


def pair_turn(x, odd_sign):
    rows, cols = x.shape
    tiles = x.reshape(rows // 8, 8, cols)
    even = lax.broadcasted_iota(jnp.int32, tiles.shape, 1) % 2 == 0
    turned = jnp.where(even, -odd_sign * pltpu.roll(tiles, 7, 1), odd_sign * pltpu.roll(tiles, 1, 1))
    return turned.reshape(rows, cols)


def project_kernel(
    ret_ref, x_hbm, e_hbm, g_ref, s_ref, eb,
    xb, acc_re, acc_im, pf, sbuf, rbuf, a1, a2,
    x_sem, e_sem, rs_send, rs_recv, ag_send, ag_recv, z_send, z_recv, w_send, w_recv,
):
    modes, freqs, half = xb.shape[0], e_hbm.shape[1], rbuf.shape[1]
    blocks = xb.shape[1] // freqs
    rows, kmax = sbuf.shape[1:]
    ma = lax.axis_index("ma")
    y = lax.axis_index("freq")
    core = lax.rem(ma, NCORE)
    z = lax.rem(ma // NCORE, NZ)
    x = ma // (NCORE * NZ)

    def x_copy(m, f, b):
        j = f * blocks + b
        return pltpu.make_async_copy(
            x_hbm.at[m, :, f, :, pl.ds(b * LANES, LANES)], xb.at[m, j], x_sem.at[m, j]
        )

    def e_copy(m, f):
        return pltpu.make_async_copy(e_hbm.at[m, f], eb.at[m, f], e_sem.at[m, f])

    for m in range(modes):
        for f in range(freqs):
            e_copy(m, f).start()
            for b in range(blocks):
                x_copy(m, f, b).start()

    z_peers = [((x * NZ + lax.rem(z + d, NZ)) * NCORE + core, lax.rem(z + d, NZ)) for d in range(NZ)]
    xs = [lax.rem(x + d, NX) for d in range(NX)]
    ys = [lax.rem(y + d, NY) for d in range(NY)]
    cs = [core, 1 - core]
    far = [2, 1, 3, 0]
    w_peers = [
        ((xs[dx] * NZ + z) * NCORE + cs[dc], ys[dy])
        for dx in far for dy in far for dc in (1, 0)
        if (dx, dy, dc) != (0, 0, 0)
    ]
    barrier = pltpu.get_barrier_semaphore()
    for peer in w_peers:
        pl.semaphore_signal(barrier, inc=1, device_id={"ma": peer[0], "freq": peer[1]}, device_id_type=MESH)
    for d in range(1, NZ):
        pl.semaphore_signal(barrier, inc=1, device_id={"ma": z_peers[d][0], "freq": y}, device_id_type=MESH)

    def rs_copy(m, h):
        t = 2 * m + h
        return pltpu.make_async_remote_copy(
            src_ref=sbuf.at[m, pl.ds(h * half, half)], dst_ref=rbuf.at[y],
            send_sem=rs_send.at[t], recv_sem=rs_recv.at[y],
            device_id={"ma": ma, "freq": t}, device_id_type=MESH,
        )

    for m in range(modes):
        for f in range(freqs):
            e_copy(m, f).wait()
            for b in range(blocks):
                x_copy(m, f, b).wait()
            lhs = jnp.concatenate(
                [xb.at[m, f * blocks + b].reshape(rows, LANES)[...] for b in range(blocks)], axis=1
            )
            d_re = jnp.dot(lhs, eb[m, f, 0], preferred_element_type=F32)
            d_im = jnp.dot(lhs, eb[m, f, 1], preferred_element_type=F32)
            if f == 0:
                acc_re[...] = d_re
                acc_im[...] = d_im
            else:
                acc_re[...] += d_re
                acc_im[...] += d_im
        proj = acc_re[...] + pair_turn(acc_im[...], -1.0)
        pf[m] = proj
        sbuf[m] = proj.astype(BF16)
        if m == 0:
            pl.semaphore_wait(barrier, len(w_peers) + NZ - 1)
        for h in range(2):
            @pl.when(2 * m + h != y)
            def _():
                rs_copy(m, h).start()

    share = pf[y // 2, pl.ds(lax.rem(y, 2) * half, half), :]
    for d in range(1, NY):
        src = ys[d]
        pltpu.make_async_remote_copy(
            src_ref=sbuf.at[0, pl.ds(0, half)], dst_ref=rbuf.at[src],
            send_sem=rs_send.at[src], recv_sem=rs_recv.at[src],
            device_id={"ma": ma, "freq": src}, device_id_type=MESH,
        ).wait_recv()
        share = share + rbuf[src].astype(F32)
    cut = ret_ref[y // 2]
    keep = (lax.broadcasted_iota(jnp.int32, (1, kmax), 1) < cut).astype(F32)
    power = keep * jnp.sum(share * share, axis=0, keepdims=True)
    count = keep * (half // 2)
    parts = kmax // LANES
    for p in range(parts):
        a1[z, pl.ds(p, 1), :] = power[:, p * LANES : (p + 1) * LANES]
        a1[z, pl.ds(parts + p, 1), :] = count[:, p * LANES : (p + 1) * LANES]

    def z_copy(d):
        return pltpu.make_async_remote_copy(
            src_ref=a1.at[z], dst_ref=a1.at[z], send_sem=z_send.at[d], recv_sem=z_recv.at[z],
            device_id={"ma": z_peers[d][0], "freq": y}, device_id_type=MESH,
        )

    for d in (4, 3, 5, 2, 6, 1, 7):
        z_copy(d).start()

    g_ref[y] = share.astype(BF16)

    def ag_copy(d):
        return pltpu.make_async_remote_copy(
            src_ref=g_ref.at[y], dst_ref=g_ref.at[y], send_sem=ag_send.at[d], recv_sem=ag_recv.at[y],
            device_id={"ma": ma, "freq": ys[d]}, device_id_type=MESH,
        )

    for d in (2, 1, 3):
        ag_copy(d).start()

    for d in range(1, NZ):
        src = z_peers[d][1]
        pltpu.make_async_remote_copy(
            src_ref=a1.at[z], dst_ref=a1.at[src], send_sem=z_send.at[d], recv_sem=z_recv.at[src],
            device_id={"ma": z_peers[d][0], "freq": y}, device_id_type=MESH,
        ).wait_recv()
    total = a1[0]
    for i in range(1, NZ):
        total = total + a1[i]

    q = (x * NY + y) * NCORE + core
    a2[q] = total

    def w_copy(i):
        return pltpu.make_async_remote_copy(
            src_ref=a2.at[q], dst_ref=a2.at[q], send_sem=w_send.at[i], recv_sem=w_recv.at[q],
            device_id={"ma": w_peers[i][0], "freq": w_peers[i][1]}, device_id_type=MESH,
        )

    for i in range(len(w_peers)):
        w_copy(i).start()
    for d in range(1, NX * NY * NCORE):
        src = lax.rem(q + d, NX * NY * NCORE)
        pltpu.make_async_remote_copy(
            src_ref=a2.at[q], dst_ref=a2.at[src], send_sem=w_send.at[d - 1], recv_sem=w_recv.at[src],
            device_id={"ma": ma, "freq": ys[1]}, device_id_type=MESH,
        ).wait_recv()
    total = a2[0]
    for i in range(1, NX * NY * NCORE):
        total = total + a2[i]
    s_ref[...] = 1.0 / jnp.sqrt(total[:parts] / jnp.maximum(total[parts:], 1.0) + 1e-06)

    for d in range(1, NY):
        src = ys[d]
        pltpu.make_async_remote_copy(
            src_ref=g_ref.at[y], dst_ref=g_ref.at[src], send_sem=ag_send.at[d], recv_sem=ag_recv.at[src],
            device_id={"ma": ma, "freq": src}, device_id_type=MESH,
        ).wait_recv()
    for m in range(modes):
        for h in range(2):
            @pl.when(2 * m + h != y)
            def _():
                rs_copy(m, h).wait_send()
    for d in range(1, NY):
        ag_copy(d).wait_send()
    for d in range(1, NZ):
        z_copy(d).wait_send()
    for i in range(len(w_peers)):
        w_copy(i).wait_send()


def filter_kernel(ret_ref, g_ref, s_ref, eb, c_ref, o_hbm, cf, ob, o_sem):
    modes, freqs = eb.shape[:2]
    blocks = ob.shape[1] // freqs
    kmax = c_ref.shape[3]
    rows = cf.shape[1]
    half = rows // 2
    parts = kmax // LANES

    def o_copy(m, f, b):
        j = f * blocks + b
        return pltpu.make_async_copy(
            ob.at[m, j], o_hbm.at[m, :, f, :, pl.ds(b * LANES, LANES)], o_sem.at[m, j]
        )

    scale = jnp.concatenate([s_ref[pl.ds(p, 1), :] for p in range(parts)], axis=1)
    for m in range(modes):
        keep = (lax.broadcasted_iota(jnp.int32, (1, kmax), 1) < ret_ref[m]).astype(F32)
        gain = keep * scale
        c = jnp.concatenate([g_ref[2 * m], g_ref[2 * m + 1]], axis=0).astype(F32) * gain
        for p in range(parts):
            cf[p] = c[:, p * LANES : (p + 1) * LANES]
        lhs_re = c.astype(BF16)
        lhs_im = pair_turn(c, 1.0).astype(BF16)
        for part in range(2):
            c_ref[m, part] = jnp.concatenate(
                [cf[p, pl.ds(part, half, stride=2), :] for p in range(parts)], axis=1
            ).astype(BF16)
        for f in range(freqs):
            dims = (((1,), (1,)), ((), ()))
            out = lax.dot_general(lhs_re, eb[m, f, 0], dims, preferred_element_type=F32)
            out = out + lax.dot_general(lhs_im, eb[m, f, 1], dims, preferred_element_type=F32)
            for b in range(blocks):
                ob.at[m, f * blocks + b].reshape(rows, LANES)[...] = out[:, b * LANES : (b + 1) * LANES].astype(BF16)
                o_copy(m, f, b).start()
    for m in range(modes):
        for f in range(freqs):
            for b in range(blocks):
                o_copy(m, f, b).wait()


def per_device(visibilities, eigenmodes, retained):
    modes, samples, freqs, _, base = visibilities.shape
    kmax = eigenmodes.shape[-1]
    blocks = base // LANES
    rows = 2 * samples
    half = rows // 2
    group = NX * NY * NCORE
    visibilities, eigenmodes, retained = (
        pltpu.with_memory_space_constraint(a, pltpu.HBM) for a in (visibilities, eigenmodes, retained)
    )
    any_spec = pl.BlockSpec(memory_space=pl.ANY)
    vmem_spec = pl.BlockSpec(memory_space=pltpu.VMEM)
    smem_spec = pl.BlockSpec(memory_space=pltpu.SMEM)
    dma = pltpu.SemaphoreType.DMA
    flops = 2 * modes * rows * freqs * 2 * base * kmax
    gathered, scale, vectors = pl.pallas_call(
        project_kernel,
        out_shape=(
            jax.ShapeDtypeStruct((NY, half, kmax), BF16),
            jax.ShapeDtypeStruct((kmax // LANES, LANES), F32),
            jax.ShapeDtypeStruct((modes, freqs, 2, base, kmax), BF16),
        ),
        in_specs=[smem_spec, any_spec, any_spec],
        out_specs=(vmem_spec, vmem_spec, vmem_spec),
        scratch_shapes=[
            pltpu.VMEM((modes, freqs * blocks, samples, 2, LANES), BF16),
            pltpu.VMEM((rows, kmax), F32),
            pltpu.VMEM((rows, kmax), F32),
            pltpu.VMEM((modes, rows, kmax), F32),
            pltpu.VMEM((modes, rows, kmax), BF16),
            pltpu.VMEM((NY, half, kmax), BF16),
            pltpu.VMEM((NZ, 2 * kmax // LANES, LANES), F32),
            pltpu.VMEM((group, 2 * kmax // LANES, LANES), F32),
            dma((modes, freqs * blocks)),
            dma((modes, freqs)),
            dma((NY,)), dma((NY,)),
            dma((NY,)), dma((NY,)),
            dma((NZ,)), dma((NZ,)),
            dma((group,)), dma((group,)),
        ],
        compiler_params=pltpu.CompilerParams(
            collective_id=0, has_side_effects=True, vmem_limit_bytes=24 << 20
        ),
        cost_estimate=pl.CostEstimate(flops=flops, bytes_accessed=8 << 20, transcendentals=0),
    )(retained, visibilities, eigenmodes)
    coefficients, filtered = pl.pallas_call(
        filter_kernel,
        out_shape=(
            jax.ShapeDtypeStruct((modes, 2, samples, kmax), BF16),
            jax.ShapeDtypeStruct((modes, samples, freqs, 2, base), BF16),
        ),
        in_specs=[smem_spec, vmem_spec, vmem_spec, vmem_spec],
        out_specs=(vmem_spec, any_spec),
        scratch_shapes=[
            pltpu.VMEM((kmax // LANES, rows, LANES), F32),
            pltpu.VMEM((modes, freqs * blocks, samples, 2, LANES), BF16),
            dma((modes, freqs * blocks)),
        ],
        compiler_params=pltpu.CompilerParams(vmem_limit_bytes=24 << 20),
        cost_estimate=pl.CostEstimate(flops=flops, bytes_accessed=8 << 20, transcendentals=0),
    )(retained, gathered, scale, vectors)
    return coefficients, filtered


def solution(mesh):
    return jax.shard_map(
        per_device,
        mesh=mesh,
        in_specs=(P("ma", None, "freq", None, None), P("ma", "freq", None, None, None), P("ma")),
        out_specs=(P("ma", None, None, None), P("ma", None, "freq", None, None)),
        check_vma=False,
    )
```

time: 148 us -> 37.6 us (0.25); the launches traced: 145 us -> 37.5 us
  other arithmetic: 41.3 us -> 0 us
  Pallas kernels: 0 us -> 36.8 us
  local copies, waits for them, and re-layouts: 34.9 us -> 0 us
  blocking collectives: 33 us -> 0 us
  matrix products: 17 us -> 0 us
  waiting for transfers between devices: 13.3 us -> 0 us
  starting transfers between devices: 5 us -> 0 us
    pallas_call x0 -> x2, Pallas kernels: none -> 36.8 us  [the longest x1 30.4 us: per_device(): pl.pallas_call(project_kernel, out_shape=(jax.ShapeDtypeStruct((NY, half,...]
    another operation x4 -> x0, other arithmetic: 34.7 us -> none
    reshape x6 -> x0, local copies, waits for them, and re-layouts: 31.1 us -> none  [the longest x1 9.18 us: per_device(): second = jnp.einsum('msk,mck->msc', coef_im, matrix, preferred_element_ty...]
    all_to_all x1 -> x0, blocking collectives: 23.1 us -> none  [copy_for_each(): lax.all_to_all(jnp.broadcast_to(x[None], (count, *x.shape)), axis, 0, 0,...]
    dot_general x4 -> x0, matrix products: 17 us -> none  [the longest x1 6.37 us: per_device(): jnp.einsum('msk,mck->msc', coef_im, matrix, preferred_element_type=jnp.fl...]
    all_to_all x1 -> x0, waiting for transfers between devices: 13.3 us -> none  [summed_on_arrival(): lax.all_to_all(pieces, axis, split_axis=0, concat_axis=0, tiled=True)]
    all_gather x1 -> x0, blocking collectives: 9.82 us -> none  [gather_turned(): filled = lax.all_gather(both, axis, axis=0, tiled=True)]
    slice x1 -> x0, other arithmetic: 5.76 us -> none  [per_device(): visibilities[:, :, :, 1, :]]
  transfers between devices with their start and end apart: 1 -> 0, of which waited for: 1 -> 0; matrix products, arithmetic and copies ran while one was open for 0% -> 0% of each run, Pallas kernels for 0% -> 0%
where the time goes in v1:
time: 37.6 us; the launch traced here: 37.5 us
  Pallas kernels  36.8 us (98%)
  between operations  0.64 us (2%)
    pallas_call x1, Pallas kernels, per_device(): pl.pallas_call(project_kernel, out_shape=(jax.ShapeDtypeStruct((NY, half,...  30.4 us
    pallas_call x1, Pallas kernels, per_device(): pl.pallas_call(filter_kernel, out_shape=(jax.ShapeDtypeStruct((modes, 2,...  6.45 us

profile of v1, /device:TPU:1, one launch (start us, length us, event | category | flops | bytes accessed | tf_op | source)
XLA Modules:
  0.0 37.5 jit_solution(963921269468264204)
XLA Ops:
  0.6 30.4 %shard_map.50 = (bf16[4,192,256]{2,1,0:T(8,128)(2,1)S(1)}, f32[2,128]{1,0:T(2,128)S(1)}, bf16[2,4,2,512,256]{4,3,2,1,0:T(8,128)(2,1)S(1)}) custom-call(s32[2]{0:T(128)} %ret_ref.3, bf16[2,192,4,2,512]{4,3,2,1,0:T(2,128)(2,1)} %x_hbm.1, bf16[2,4,2,512,256]{4,3,2,1,0:T(8,128)(2,1)} %e_hbm.1), custom_call_target="tpu_custom_call" | custom-call | flops 1610612736 | bytes 8388608 | tf_op jit(solution)/shard_map/pallas_call | solution.py:247
  31.0 6.4 %shard_map.51 = (bf16[2,2,192,256]{3,2,1,0:T(8,128)(2,1)}, bf16[2,192,4,2,512]{4,3,2,1,0:T(2,128)(2,1)}) custom-call(s32[2]{0:T(128)} %ret_ref.3, bf16[4,192,256]{2,1,0:T(8,128)(2,1)S(1)} %get-tuple-element.5.g_ref, f32[2,128]{1,0:T(2,128)S(1)} %get-tuple-element.6.s_ref, bf16[2,4,2,512,256]{4,3,2,1,0:T(8,128)(2,1)S(1)} %get-tuple-element.7.eb), custom_call_target="tpu_custom_call" | custom-call | flops 1610612736 | bytes 8388608 | tf_op jit(solution)/shard_map/pallas_call | solution.py:277

commit v2 on v1

--- a/solution.py
+++ b/solution.py
@@ -23,8 +23,8 @@
 
 def project_kernel(
     ret_ref, x_hbm, e_hbm, g_ref, s_ref, eb,
-    xb, acc_re, acc_im, pf, sbuf, rbuf, a1, a2,
-    x_sem, e_sem, rs_send, rs_recv, ag_send, ag_recv, z_send, z_recv, w_send, w_recv,
+    xt, xb, acc_re, acc_im, pf, sbuf, rbuf, a1, a2,
+    x_sem, t_sem, e_sem, rs_send, rs_recv, ag_send, ag_recv, z_send, z_recv, w_send, w_recv,
 ):
     modes, freqs, half = xb.shape[0], e_hbm.shape[1], rbuf.shape[1]
     blocks = xb.shape[1] // freqs
@@ -38,8 +38,18 @@
     def x_copy(m, f, b):
         j = f * blocks + b
         return pltpu.make_async_copy(
-            x_hbm.at[m, :, f, :, pl.ds(b * LANES, LANES)], xb.at[m, j], x_sem.at[m, j]
-        )
+            x_hbm.at[m, :, f, :, pl.ds(b * LANES, LANES)], xt.at[m, j], x_sem.at[m, j]
+        )
+
+    def t_copy(m, f, b):
+        j = f * blocks + b
+        return pltpu.make_async_copy(xt.at[m, j].reshape(rows, LANES), xb.at[m, j], t_sem.at[m, j])
+
+    def take(u):
+        m, f = divmod(u, freqs)
+        for b in range(blocks):
+            x_copy(m, f, b).wait()
+            t_copy(m, f, b).start()
 
     def e_copy(m, f):
         return pltpu.make_async_copy(e_hbm.at[m, f], eb.at[m, f], e_sem.at[m, f])
@@ -76,12 +86,15 @@
 
     for m in range(modes):
         for f in range(freqs):
+            u = m * freqs + f
+            if u == 0:
+                take(0)
+            if u + 1 < modes * freqs:
+                take(u + 1)
             e_copy(m, f).wait()
             for b in range(blocks):
-                x_copy(m, f, b).wait()
-            lhs = jnp.concatenate(
-                [xb.at[m, f * blocks + b].reshape(rows, LANES)[...] for b in range(blocks)], axis=1
-            )
+                t_copy(m, f, b).wait()
+            lhs = jnp.concatenate([xb[m, f * blocks + b] for b in range(blocks)], axis=1)
             d_re = jnp.dot(lhs, eb[m, f, 0], preferred_element_type=F32)
             d_im = jnp.dot(lhs, eb[m, f, 1], preferred_element_type=F32)
             if f == 0:
@@ -189,7 +202,7 @@
         w_copy(i).wait_send()
 
 
-def filter_kernel(ret_ref, g_ref, s_ref, eb, c_ref, o_hbm, cf, ob, o_sem):
+def filter_kernel(ret_ref, g_ref, s_ref, eb, c_ref, o_hbm, cf, ob, ot, t_sem, o_sem):
     modes, freqs = eb.shape[:2]
     blocks = ob.shape[1] // freqs
     kmax = c_ref.shape[3]
@@ -200,8 +213,18 @@
     def o_copy(m, f, b):
         j = f * blocks + b
         return pltpu.make_async_copy(
-            ob.at[m, j], o_hbm.at[m, :, f, :, pl.ds(b * LANES, LANES)], o_sem.at[m, j]
-        )
+            ot.at[m, j], o_hbm.at[m, :, f, :, pl.ds(b * LANES, LANES)], o_sem.at[m, j]
+        )
+
+    def t_copy(m, f, b):
+        j = f * blocks + b
+        return pltpu.make_async_copy(ob.at[m, j], ot.at[m, j].reshape(rows, LANES), t_sem.at[m, j])
+
+    def give(u):
+        m, f = divmod(u, freqs)
+        for b in range(blocks):
+            t_copy(m, f, b).wait()
+            o_copy(m, f, b).start()
 
     scale = jnp.concatenate([s_ref[pl.ds(p, 1), :] for p in range(parts)], axis=1)
     for m in range(modes):
@@ -221,8 +244,11 @@
             out = lax.dot_general(lhs_re, eb[m, f, 0], dims, preferred_element_type=F32)
             out = out + lax.dot_general(lhs_im, eb[m, f, 1], dims, preferred_element_type=F32)
             for b in range(blocks):
-                ob.at[m, f * blocks + b].reshape(rows, LANES)[...] = out[:, b * LANES : (b + 1) * LANES].astype(BF16)
-                o_copy(m, f, b).start()
+                ob[m, f * blocks + b] = out[:, b * LANES : (b + 1) * LANES].astype(BF16)
+                t_copy(m, f, b).start()
+            if m + f > 0:
+                give(m * freqs + f - 1)
+    give(modes * freqs - 1)
     for m in range(modes):
         for f in range(freqs):
             for b in range(blocks):
@@ -255,6 +281,7 @@
         out_specs=(vmem_spec, vmem_spec, vmem_spec),
         scratch_shapes=[
             pltpu.VMEM((modes, freqs * blocks, samples, 2, LANES), BF16),
+            pltpu.VMEM((modes, freqs * blocks, rows, LANES), BF16),
             pltpu.VMEM((rows, kmax), F32),
             pltpu.VMEM((rows, kmax), F32),
             pltpu.VMEM((modes, rows, kmax), F32),
@@ -262,6 +289,7 @@
             pltpu.VMEM((NY, half, kmax), BF16),
             pltpu.VMEM((NZ, 2 * kmax // LANES, LANES), F32),
             pltpu.VMEM((group, 2 * kmax // LANES, LANES), F32),
+            dma((modes, freqs * blocks)),
             dma((modes, freqs * blocks)),
             dma((modes, freqs)),
             dma((NY,)), dma((NY,)),
@@ -284,7 +312,9 @@
         out_specs=(vmem_spec, any_spec),
         scratch_shapes=[
             pltpu.VMEM((kmax // LANES, rows, LANES), F32),
+            pltpu.VMEM((modes, freqs * blocks, rows, LANES), BF16),
             pltpu.VMEM((modes, freqs * blocks, samples, 2, LANES), BF16),
+            dma((modes, freqs * blocks)),
             dma((modes, freqs * blocks)),
         ],
         compiler_params=pltpu.CompilerParams(vmem_limit_bytes=24 << 20),

time: 37.6 us -> 44.2 us (1.18)
  Pallas kernels: 36.8 us -> 43.5 us
    pallas_call x1, Pallas kernels: 6.45 us -> 10.4 us  [per_device(): pl.pallas_call(filter_kernel, out_shape=(jax.ShapeDtypeStruct((modes, 2,...]
    pallas_call x1, Pallas kernels: 30.4 us -> 33.1 us  [per_device(): pl.pallas_call(project_kernel, out_shape=(jax.ShapeDtypeStruct((NY, half,...]
where the time goes in v2:
time: 44.2 us; the launch traced here: 44.1 us
  Pallas kernels  43.5 us (98%)
  between operations  0.64 us (1%)
    pallas_call x1, Pallas kernels, per_device(): pl.pallas_call(project_kernel, out_shape=(jax.ShapeDtypeStruct((NY, half,...  33.1 us
    pallas_call x1, Pallas kernels, per_device(): pl.pallas_call(filter_kernel, out_shape=(jax.ShapeDtypeStruct((modes, 2,...  10.4 us

profile of v2, /device:TPU:1, one launch (start us, length us, event | category | flops | bytes accessed | tf_op | source)
XLA Modules:
  0.0 44.1 jit_solution(8326866173530488344)
XLA Ops:
  0.6 33.1 %shard_map.50 = (bf16[4,192,256]{2,1,0:T(8,128)(2,1)S(1)}, f32[2,128]{1,0:T(2,128)S(1)}, bf16[2,4,2,512,256]{4,3,2,1,0:T(8,128)(2,1)S(1)}) custom-call(s32[2]{0:T(128)} %ret_ref.3, bf16[2,192,4,2,512]{4,3,2,1,0:T(2,128)(2,1)} %x_hbm.1, bf16[2,4,2,512,256]{4,3,2,1,0:T(8,128)(2,1)} %e_hbm.1), custom_call_target="tpu_custom_call" | custom-call | flops 1610612736 | bytes 8388608 | tf_op jit(solution)/shard_map/pallas_call | solution.py:273
  33.7 10.4 %shard_map.51 = (bf16[2,2,192,256]{3,2,1,0:T(8,128)(2,1)}, bf16[2,192,4,2,512]{4,3,2,1,0:T(2,128)(2,1)}) custom-call(s32[2]{0:T(128)} %ret_ref.3, bf16[4,192,256]{2,1,0:T(8,128)(2,1)S(1)} %get-tuple-element.5.g_ref, f32[2,128]{1,0:T(2,128)S(1)} %get-tuple-element.6.s_ref, bf16[2,4,2,512,256]{4,3,2,1,0:T(8,128)(2,1)S(1)} %get-tuple-element.7.eb), custom_call_target="tpu_custom_call" | custom-call | flops 1610612736 | bytes 8388608 | tf_op jit(solution)/shard_map/pallas_call | solution.py:305

commit v3 on v1

v3 whole, which is shorter than its diff:
```python
import functools

import jax
import jax.numpy as jnp
from jax import lax
from jax.experimental import pallas as pl
from jax.experimental.pallas import tpu as pltpu
from jax.sharding import PartitionSpec as P

MESH = pl.DeviceIdType.MESH
BF16, F32 = jnp.bfloat16, jnp.float32
NX, NZ, NCORE, NY = 4, 8, 2, 4
LANES = 128


def project_kernel(
    ret_hbm, x_hbm, e_hbm, g_ref, s_ref, eb,
    ret_ref, xb, acc_re, acc_im, pf, sbuf, rbuf, a1, a2,
    ret_sem, x_sem, e_sem, rs_send, rs_recv, ag_send, ag_recv, z_send, z_recv, w_send, w_recv,
):
    modes, freqs, _, base, kmax = eb.shape
    samples = pf.shape[2]
    half = samples // 2
    parts = kmax // LANES
    ma = lax.axis_index("ma")
    y = lax.axis_index("freq")
    core = lax.rem(ma, NCORE)
    z = lax.rem(ma // NCORE, NZ)
    x = ma // (NCORE * NZ)

    def x_copy(m, f):
        return pltpu.make_async_copy(x_hbm.at[m, :, f], xb.at[m, f], x_sem.at[m, f])

    def e_copy(m, f):
        return pltpu.make_async_copy(e_hbm.at[m, f], eb.at[m, f], e_sem.at[m, f])

    order = (1 - y // 2, y // 2)
    for m in order:
        for f in range(freqs):
            x_copy(m, f).start()
            e_copy(m, f).start()
    ret_copy = pltpu.make_async_copy(ret_hbm, ret_ref, ret_sem)
    ret_copy.start()

    z_peers = [((x * NZ + lax.rem(z + d, NZ)) * NCORE + core, lax.rem(z + d, NZ)) for d in range(NZ)]
    xs = [lax.rem(x + d, NX) for d in range(NX)]
    ys = [lax.rem(y + d, NY) for d in range(NY)]
    cs = [core, 1 - core]
    far = [2, 1, 3, 0]
    w_peers = [
        ((xs[dx] * NZ + z) * NCORE + cs[dc], ys[dy])
        for dx in far for dy in far for dc in (1, 0)
        if (dx, dy, dc) != (0, 0, 0)
    ]
    barrier = pltpu.get_barrier_semaphore()
    for peer in w_peers:
        pl.semaphore_signal(barrier, inc=1, device_id={"ma": peer[0], "freq": peer[1]}, device_id_type=MESH)
    for d in range(1, NZ):
        pl.semaphore_signal(barrier, inc=1, device_id={"ma": z_peers[d][0], "freq": y}, device_id_type=MESH)

    def rs_copy(i, t):
        return pltpu.make_async_remote_copy(
            src_ref=sbuf.at[i], dst_ref=rbuf.at[y], send_sem=rs_send.at[i], recv_sem=rs_recv.at[y],
            device_id={"ma": ma, "freq": t}, device_id_type=MESH,
        )

    mine = lax.rem(y, 2)
    rs_copies = (rs_copy(0, 2 * order[0] + mine), rs_copy(1, 2 * order[0] + 1 - mine), rs_copy(2, 2 * order[1] + 1 - mine))

    def hand_over(i, slot, h):
        for c in range(2):
            sbuf[i, c] = pf[slot, c, pl.ds(pl.multiple_of(h * half, 32), half), :].astype(BF16)
        rs_copies[i].start()

    for slot in range(modes):
        m = order[slot]
        for f in range(freqs):
            x_copy(m, f).wait()
            e_copy(m, f).wait()
            lhs = xb[m, f].reshape(2 * samples, base)
            for c, acc in ((0, acc_re), (1, acc_im)):
                d = jnp.dot(lhs, eb[m, f, c], preferred_element_type=F32)
                for p in range(parts):
                    piece = d[:, p * LANES : (p + 1) * LANES]
                    acc[slot, p] = piece if f == 0 else acc[slot, p] + piece
        even, odd = pl.ds(0, samples, stride=2), pl.ds(1, samples, stride=2)
        for p in range(parts):
            lanes = slice(p * LANES, (p + 1) * LANES)
            pf[slot, 0, :, lanes] = acc_re[slot, p, even, :] + acc_im[slot, p, odd, :]
            pf[slot, 1, :, lanes] = acc_re[slot, p, odd, :] - acc_im[slot, p, even, :]
        if slot == 0:
            pl.semaphore_wait(barrier, len(w_peers) + NZ - 1)
            hand_over(0, 0, mine)
            hand_over(1, 0, 1 - mine)
        else:
            hand_over(2, 1, 1 - mine)

    share = pf[1, :, pl.ds(pl.multiple_of(mine * half, 32), half), :]
    for d in range(1, NY):
        src = ys[d]
        pltpu.make_async_remote_copy(
            src_ref=sbuf.at[0], dst_ref=rbuf.at[src],
            send_sem=rs_send.at[d - 1], recv_sem=rs_recv.at[src],
            device_id={"ma": ma, "freq": src}, device_id_type=MESH,
        ).wait_recv()
        share = share + rbuf[src].astype(F32)
    ret_copy.wait()
    ranks = lax.broadcasted_iota(jnp.int32, (1, kmax), 1)
    keep = (ranks < ret_ref[y // 2]).astype(F32)
    power = keep * jnp.sum(share[0] * share[0] + share[1] * share[1], axis=0, keepdims=True)
    count = keep * half
    for p in range(parts):
        a1[z, pl.ds(p, 1), :] = power[:, p * LANES : (p + 1) * LANES]
        a1[z, pl.ds(parts + p, 1), :] = count[:, p * LANES : (p + 1) * LANES]

    def z_copy(d):
        return pltpu.make_async_remote_copy(
            src_ref=a1.at[z], dst_ref=a1.at[z], send_sem=z_send.at[d], recv_sem=z_recv.at[z],
            device_id={"ma": z_peers[d][0], "freq": y}, device_id_type=MESH,
        )

    for d in (4, 3, 5, 2, 6, 1, 7):
        z_copy(d).start()

    g_ref[y] = share.astype(BF16)

    def ag_copy(d):
        return pltpu.make_async_remote_copy(
            src_ref=g_ref.at[y], dst_ref=g_ref.at[y], send_sem=ag_send.at[d], recv_sem=ag_recv.at[y],
            device_id={"ma": ma, "freq": ys[d]}, device_id_type=MESH,
        )

    for d in (2, 1, 3):
        ag_copy(d).start()

    for d in range(1, NZ):
        src = z_peers[d][1]
        pltpu.make_async_remote_copy(
            src_ref=a1.at[z], dst_ref=a1.at[src], send_sem=z_send.at[d], recv_sem=z_recv.at[src],
            device_id={"ma": z_peers[d][0], "freq": y}, device_id_type=MESH,
        ).wait_recv()
    total = a1[0]
    for i in range(1, NZ):
        total = total + a1[i]

    q = (x * NY + y) * NCORE + core
    a2[q] = total

    def w_copy(i):
        return pltpu.make_async_remote_copy(
            src_ref=a2.at[q], dst_ref=a2.at[q], send_sem=w_send.at[i], recv_sem=w_recv.at[q],
            device_id={"ma": w_peers[i][0], "freq": w_peers[i][1]}, device_id_type=MESH,
        )

    for i in range(len(w_peers)):
        w_copy(i).start()
    for d in range(1, NX * NY * NCORE):
        src = lax.rem(q + d, NX * NY * NCORE)
        pltpu.make_async_remote_copy(
            src_ref=a2.at[q], dst_ref=a2.at[src], send_sem=w_send.at[d - 1], recv_sem=w_recv.at[src],
            device_id={"ma": ma, "freq": ys[1]}, device_id_type=MESH,
        ).wait_recv()
    total = a2[0]
    for i in range(1, NX * NY * NCORE):
        total = total + a2[i]
    scale = 1.0 / jnp.sqrt(total[:parts] / jnp.maximum(total[parts:], 1.0) + 1e-06)
    scale = jnp.concatenate([scale[p : p + 1, :] for p in range(parts)], axis=1)
    for m in range(modes):
        s_ref[pl.ds(m, 1), :] = (ranks < ret_ref[m]).astype(F32) * scale

    for d in range(1, NY):
        src = ys[d]
        pltpu.make_async_remote_copy(
            src_ref=g_ref.at[y], dst_ref=g_ref.at[src], send_sem=ag_send.at[d], recv_sem=ag_recv.at[src],
            device_id={"ma": ma, "freq": src}, device_id_type=MESH,
        ).wait_recv()
    for copy in rs_copies:
        copy.wait_send()
    for d in range(1, NY):
        ag_copy(d).wait_send()
    for d in range(1, NZ):
        z_copy(d).wait_send()
    for i in range(len(w_peers)):
        w_copy(i).wait_send()


def filter_kernel(g_ref, s_ref, eb, c_hbm, o_hbm, cb, of, ob, c_sem, o_sem):
    modes, freqs, _, base, kmax = eb.shape
    samples = cb.shape[2]
    blocks = base // LANES
    stride = 2 * freqs
    wide = 2 * LANES

    def o_copy(m, b):
        slab = o_hbm.at[m].reshape(samples * stride, base).at[:, pl.ds(b * LANES, LANES)]
        return pltpu.make_async_copy(ob.at[m, b], slab, o_sem.at[m, b])

    def c_copy(m):
        return pltpu.make_async_copy(cb.at[m], c_hbm.at[m], c_sem.at[m])

    for m in range(modes):
        gain = s_ref[pl.ds(m, 1), :]
        re, im = (
            (jnp.concatenate([g_ref[2 * m, c], g_ref[2 * m + 1, c]], axis=0).astype(F32) * gain).astype(BF16)
            for c in range(2)
        )
        cb[m, 0] = re
        cb[m, 1] = im
        c_copy(m).start()
        lhs = jnp.concatenate(
            [jnp.concatenate([re, -im], axis=1), jnp.concatenate([im, re], axis=1)], axis=0
        )
        for p in range(blocks // 2):
            for f in range(freqs):
                rhs = jnp.concatenate([eb[m, f, c, p * wide : (p + 1) * wide, :] for c in range(2)], axis=1)
                out = lax.dot_general(lhs, rhs, (((1,), (1,)), ((), ())), preferred_element_type=F32)
                for c in range(2):
                    for i in range(2):
                        of[m, 2 * p + i, pl.ds(2 * f + c, samples, stride=stride), :] = out[
                            c * samples : (c + 1) * samples, i * LANES : (i + 1) * LANES
                        ]
            for b in (2 * p, 2 * p + 1):
                ob[m, b] = of[m, b].astype(BF16)
                o_copy(m, b).start()
    for m in range(modes):
        c_copy(m).wait()
        for b in range(blocks):
            o_copy(m, b).wait()


def per_device(visibilities, eigenmodes, retained):
    modes, samples, freqs, _, base = visibilities.shape
    kmax = eigenmodes.shape[-1]
    blocks = base // LANES
    rows = 2 * samples
    half = samples // 2
    slab = samples * freqs * 2
    group = NX * NY * NCORE
    visibilities, eigenmodes, retained = (
        pltpu.with_memory_space_constraint(a, pltpu.HBM) for a in (visibilities, eigenmodes, retained)
    )
    any_spec = pl.BlockSpec(memory_space=pl.ANY)
    vmem_spec = pl.BlockSpec(memory_space=pltpu.VMEM)
    dma = pltpu.SemaphoreType.DMA
    flops = 2 * modes * rows * freqs * 2 * base * kmax
    gathered, scale, vectors = pl.pallas_call(
        project_kernel,
        out_shape=(
            jax.ShapeDtypeStruct((NY, 2, half, kmax), BF16),
            jax.ShapeDtypeStruct((modes, kmax), F32),
            jax.ShapeDtypeStruct((modes, freqs, 2, base, kmax), BF16),
        ),
        in_specs=[any_spec, any_spec, any_spec],
        out_specs=(vmem_spec, vmem_spec, vmem_spec),
        scratch_shapes=[
            pltpu.SMEM((modes,), jnp.int32),
            pltpu.VMEM((modes, freqs, samples, 2, base), BF16),
            pltpu.VMEM((modes, kmax // LANES, rows, LANES), F32),
            pltpu.VMEM((modes, kmax // LANES, rows, LANES), F32),
            pltpu.VMEM((modes, 2, samples, kmax), F32),
            pltpu.VMEM((NY - 1, 2, half, kmax), BF16),
            pltpu.VMEM((NY, 2, half, kmax), BF16),
            pltpu.VMEM((NZ, 2 * kmax // LANES, LANES), F32),
            pltpu.VMEM((group, 2 * kmax // LANES, LANES), F32),
            dma,
            dma((modes, freqs)),
            dma((modes, freqs)),
            dma((NY - 1,)), dma((NY,)),
            dma((NY,)), dma((NY,)),
            dma((NZ,)), dma((NZ,)),
            dma((group,)), dma((group,)),
        ],
        compiler_params=pltpu.CompilerParams(
            collective_id=0, has_side_effects=True, vmem_limit_bytes=32 << 20
        ),
        cost_estimate=pl.CostEstimate(flops=flops, bytes_accessed=8 << 20, transcendentals=0),
    )(retained, visibilities, eigenmodes)
    coefficients, filtered = pl.pallas_call(
        filter_kernel,
        out_shape=(
            jax.ShapeDtypeStruct((modes, 2, samples, kmax), BF16),
            jax.ShapeDtypeStruct((modes, samples, freqs, 2, base), BF16),
        ),
        in_specs=[vmem_spec, vmem_spec, vmem_spec],
        out_specs=(any_spec, any_spec),
        scratch_shapes=[
            pltpu.VMEM((modes, 2, samples, kmax), BF16),
            pltpu.VMEM((modes, blocks, slab, LANES), F32),
            pltpu.VMEM((modes, blocks, slab, LANES), BF16),
            dma((modes,)),
            dma((modes, blocks)),
        ],
        compiler_params=pltpu.CompilerParams(vmem_limit_bytes=32 << 20),
        cost_estimate=pl.CostEstimate(flops=flops, bytes_accessed=8 << 20, transcendentals=0),
    )(gathered, scale, vectors)
    return coefficients, filtered


def solution(mesh):
    return jax.shard_map(
        per_device,
        mesh=mesh,
        in_specs=(P("ma", None, "freq", None, None), P("ma", "freq", None, None, None), P("ma")),
        out_specs=(P("ma", None, None, None), P("ma", None, "freq", None, None)),
        check_vma=False,
    )
```

time: 37.6 us -> 31.9 us (0.85)
  Pallas kernels: 36.8 us -> 31.1 us
    pallas_call x1, Pallas kernels: 6.45 us -> 3.51 us  [per_device(): pl.pallas_call(filter_kernel, out_shape=(jax.ShapeDtypeStruct((modes, 2,...]
    pallas_call x1, Pallas kernels: 30.4 us -> 27.6 us  [per_device(): pl.pallas_call(project_kernel, out_shape=(jax.ShapeDtypeStruct((NY, 2, ha...]
where the time goes in v3:
time: 31.9 us; the launch traced here: 31.8 us
  Pallas kernels  31.1 us (97%)
  between operations  0.64 us (2%)
    pallas_call x1, Pallas kernels, per_device(): pl.pallas_call(project_kernel, out_shape=(jax.ShapeDtypeStruct((NY, 2, ha...  27.6 us
    pallas_call x1, Pallas kernels, per_device(): pl.pallas_call(filter_kernel, out_shape=(jax.ShapeDtypeStruct((modes, 2,...  3.51 us

profile of v3, /device:TPU:1, one launch (start us, length us, event | category | flops | bytes accessed | tf_op | source)
XLA Modules:
  0.0 31.8 jit_solution(12396412603763689973)
XLA Ops:
  0.6 27.6 %shard_map.50 = (bf16[4,2,96,256]{3,2,1,0:T(8,128)(2,1)S(1)}, f32[2,256]{1,0:T(2,128)S(1)}, bf16[2,4,2,512,256]{4,3,2,1,0:T(8,128)(2,1)S(1)}) custom-call(s32[2]{0:T(128)} %ret_hbm.1, bf16[2,192,4,2,512]{4,3,2,1,0:T(2,128)(2,1)} %x_hbm.1, bf16[2,4,2,512,256]{4,3,2,1,0:T(8,128)(2,1)} %e_hbm.1), custom_call_target="tpu_custom_call" | custom-call | flops 1610612736 | bytes 8388608 | tf_op jit(solution)/shard_map/pallas_call | solution.py:246
  28.3 3.5 %shard_map.51 = (bf16[2,2,192,256]{3,2,1,0:T(8,128)(2,1)}, bf16[2,192,4,2,512]{4,3,2,1,0:T(2,128)(2,1)}) custom-call(bf16[4,2,96,256]{3,2,1,0:T(8,128)(2,1)S(1)} %get-tuple-element.5.g_ref, f32[2,256]{1,0:T(2,128)S(1)} %get-tuple-element.6.s_ref, bf16[2,4,2,512,256]{4,3,2,1,0:T(8,128)(2,1)S(1)} %get-tuple-element.7.eb), custom_call_target="tpu_custom_call" | custom-call | flops 1610612736 | bytes 8388608 | tf_op jit(solution)/shard_map/pallas_call | solution.py:278

commit v4 on v3

--- a/solution.py
+++ b/solution.py
@@ -15,12 +15,12 @@
 
 def project_kernel(
     ret_hbm, x_hbm, e_hbm, g_ref, s_ref, eb,
-    ret_ref, xb, acc_re, acc_im, pf, sbuf, rbuf, a1, a2,
-    ret_sem, x_sem, e_sem, rs_send, rs_recv, ag_send, ag_recv, z_send, z_recv, w_send, w_recv,
+    ret_ref, xb, xh, acc_re, acc_im, pf, sbuf, rbuf, a1, a2,
+    ret_sem, x_sem, xh_sem, e_sem, rs_send, rs_recv, ag_send, ag_recv, z_send, z_recv, w_send, w_recv,
 ):
     modes, freqs, _, base, kmax = eb.shape
-    samples = pf.shape[2]
-    half = samples // 2
+    half = pf.shape[1]
+    samples = 2 * half
     parts = kmax // LANES
     ma = lax.axis_index("ma")
     y = lax.axis_index("freq")
@@ -28,17 +28,27 @@
     z = lax.rem(ma // NCORE, NZ)
     x = ma // (NCORE * NZ)
 
-    def x_copy(m, f):
-        return pltpu.make_async_copy(x_hbm.at[m, :, f], xb.at[m, f], x_sem.at[m, f])
+    mine = lax.rem(y, 2)
+    first, second = 1 - y // 2, y // 2
+
+    def x_copy(f):
+        return pltpu.make_async_copy(x_hbm.at[first, :, f], xb.at[f], x_sem.at[f])
+
+    def xh_copy(own, f):
+        start = pl.multiple_of((mine if own else 1 - mine) * half, half)
+        return pltpu.make_async_copy(x_hbm.at[second, pl.ds(start, half), f], xh.at[own, f], xh_sem.at[own, f])
 
     def e_copy(m, f):
         return pltpu.make_async_copy(e_hbm.at[m, f], eb.at[m, f], e_sem.at[m, f])
 
-    order = (1 - y // 2, y // 2)
-    for m in order:
-        for f in range(freqs):
-            x_copy(m, f).start()
-            e_copy(m, f).start()
+    for f in range(freqs):
+        x_copy(f).start()
+        e_copy(first, f).start()
+    for f in range(freqs):
+        xh_copy(0, f).start()
+        e_copy(second, f).start()
+    for f in range(freqs):
+        xh_copy(1, f).start()
     ret_copy = pltpu.make_async_copy(ret_hbm, ret_ref, ret_sem)
     ret_copy.start()
 
@@ -58,44 +68,62 @@
     for d in range(1, NZ):
         pl.semaphore_signal(barrier, inc=1, device_id={"ma": z_peers[d][0], "freq": y}, device_id_type=MESH)
 
-    def rs_copy(i, t):
+    def rs_copy(i, part, t):
         return pltpu.make_async_remote_copy(
-            src_ref=sbuf.at[i], dst_ref=rbuf.at[y], send_sem=rs_send.at[i], recv_sem=rs_recv.at[y],
+            src_ref=sbuf.at[part], dst_ref=rbuf.at[y], send_sem=rs_send.at[i], recv_sem=rs_recv.at[y],
             device_id={"ma": ma, "freq": t}, device_id_type=MESH,
         )
 
-    mine = lax.rem(y, 2)
-    rs_copies = (rs_copy(0, 2 * order[0] + mine), rs_copy(1, 2 * order[0] + 1 - mine), rs_copy(2, 2 * order[1] + 1 - mine))
-
-    def hand_over(i, slot, h):
-        for c in range(2):
-            sbuf[i, c] = pf[slot, c, pl.ds(pl.multiple_of(h * half, 32), half), :].astype(BF16)
-        rs_copies[i].start()
-
-    for slot in range(modes):
-        m = order[slot]
-        for f in range(freqs):
-            x_copy(m, f).wait()
-            e_copy(m, f).wait()
-            lhs = xb[m, f].reshape(2 * samples, base)
-            for c, acc in ((0, acc_re), (1, acc_im)):
-                d = jnp.dot(lhs, eb[m, f, c], preferred_element_type=F32)
-                for p in range(parts):
-                    piece = d[:, p * LANES : (p + 1) * LANES]
-                    acc[slot, p] = piece if f == 0 else acc[slot, p] + piece
-        even, odd = pl.ds(0, samples, stride=2), pl.ds(1, samples, stride=2)
+    rs_copies = (
+        rs_copy(0, mine, 2 * first + mine),
+        rs_copy(1, 1 - mine, 2 * first + 1 - mine),
+        rs_copy(2, 2, 2 * second + 1 - mine),
+    )
+
+    def project(unit, m, f, lhs):
+        count = lhs.shape[0]
+        for c, acc in ((0, acc_re), (1, acc_im)):
+            d = jnp.dot(lhs, eb[m, f, c], preferred_element_type=F32)
+            for p in range(parts):
+                piece = d[:, p * LANES : (p + 1) * LANES]
+                acc[unit, p, :count] = piece if f == 0 else acc[unit, p, :count] + piece
+
+    def combine(unit, count, put):
+        even, odd = pl.ds(0, count, stride=2), pl.ds(1, count, stride=2)
         for p in range(parts):
             lanes = slice(p * LANES, (p + 1) * LANES)
-            pf[slot, 0, :, lanes] = acc_re[slot, p, even, :] + acc_im[slot, p, odd, :]
-            pf[slot, 1, :, lanes] = acc_re[slot, p, odd, :] - acc_im[slot, p, even, :]
-        if slot == 0:
-            pl.semaphore_wait(barrier, len(w_peers) + NZ - 1)
-            hand_over(0, 0, mine)
-            hand_over(1, 0, 1 - mine)
-        else:
-            hand_over(2, 1, 1 - mine)
-
-    share = pf[1, :, pl.ds(pl.multiple_of(mine * half, 32), half), :]
+            put(0, lanes, acc_re[unit, p, even, :] + acc_im[unit, p, odd, :])
+            put(1, lanes, acc_re[unit, p, odd, :] - acc_im[unit, p, even, :])
+
+    def put_halves(c, lanes, value):
+        for h in range(2):
+            sbuf[h, c, :, lanes] = value[h * half : (h + 1) * half].astype(BF16)
+
+    def put_partner(c, lanes, value):
+        sbuf[2, c, :, lanes] = value.astype(BF16)
+
+    def put_own(c, lanes, value):
+        pf[c, :, lanes] = value
+
+    for f in range(freqs):
+        x_copy(f).wait()
+        e_copy(first, f).wait()
+        project(0, first, f, xb[f].reshape(2 * samples, base))
+    combine(0, samples, put_halves)
+    pl.semaphore_wait(barrier, len(w_peers) + NZ - 1)
+    rs_copies[0].start()
+    rs_copies[1].start()
+    for f in range(freqs):
+        xh_copy(0, f).wait()
+        e_copy(second, f).wait()
+        project(1, second, f, xh[0, f].reshape(samples, base))
+    combine(1, half, put_partner)
+    rs_copies[2].start()
+    for f in range(freqs):
+        xh_copy(1, f).wait()
+        project(2, second, f, xh[1, f].reshape(samples, base))
+    combine(2, half, put_own)
+    share = pf[...]
     for d in range(1, NY):
         src = ys[d]
         pltpu.make_async_remote_copy(
@@ -115,7 +143,7 @@
 
     def z_copy(d):
         return pltpu.make_async_remote_copy(
-            src_ref=a1.at[z], dst_ref=a1.at[z], send_sem=z_send.at[d], recv_sem=z_recv.at[z],
+            src_ref=a1.at[z], dst_ref=a1.at[z], send_sem=z_send, recv_sem=z_recv,
             device_id={"ma": z_peers[d][0], "freq": y}, device_id_type=MESH,
         )
 
@@ -133,12 +161,10 @@
     for d in (2, 1, 3):
         ag_copy(d).start()
 
-    for d in range(1, NZ):
-        src = z_peers[d][1]
-        pltpu.make_async_remote_copy(
-            src_ref=a1.at[z], dst_ref=a1.at[src], send_sem=z_send.at[d], recv_sem=z_recv.at[src],
-            device_id={"ma": z_peers[d][0], "freq": y}, device_id_type=MESH,
-        ).wait_recv()
+    def settle(ref, count, sem):
+        pltpu.make_async_copy(ref.at[pl.ds(0, count)], ref.at[pl.ds(0, count)], sem).wait()
+
+    settle(a1, NZ - 1, z_recv)
     total = a1[0]
     for i in range(1, NZ):
         total = total + a1[i]
@@ -148,18 +174,13 @@
 
     def w_copy(i):
         return pltpu.make_async_remote_copy(
-            src_ref=a2.at[q], dst_ref=a2.at[q], send_sem=w_send.at[i], recv_sem=w_recv.at[q],
+            src_ref=a2.at[q], dst_ref=a2.at[q], send_sem=w_send, recv_sem=w_recv,
             device_id={"ma": w_peers[i][0], "freq": w_peers[i][1]}, device_id_type=MESH,
         )
 
     for i in range(len(w_peers)):
         w_copy(i).start()
-    for d in range(1, NX * NY * NCORE):
-        src = lax.rem(q + d, NX * NY * NCORE)
-        pltpu.make_async_remote_copy(
-            src_ref=a2.at[q], dst_ref=a2.at[src], send_sem=w_send.at[d - 1], recv_sem=w_recv.at[src],
-            device_id={"ma": ma, "freq": ys[1]}, device_id_type=MESH,
-        ).wait_recv()
+    settle(a2, len(w_peers), w_recv)
     total = a2[0]
     for i in range(1, NX * NY * NCORE):
         total = total + a2[i]
@@ -178,10 +199,8 @@
         copy.wait_send()
     for d in range(1, NY):
         ag_copy(d).wait_send()
-    for d in range(1, NZ):
-        z_copy(d).wait_send()
-    for i in range(len(w_peers)):
-        w_copy(i).wait_send()
+    settle(a1, NZ - 1, z_send)
+    settle(a2, len(w_peers), w_send)
 
 
 def filter_kernel(g_ref, s_ref, eb, c_hbm, o_hbm, cb, of, ob, c_sem, o_sem):
@@ -254,21 +273,23 @@
         out_specs=(vmem_spec, vmem_spec, vmem_spec),
         scratch_shapes=[
             pltpu.SMEM((modes,), jnp.int32),
-            pltpu.VMEM((modes, freqs, samples, 2, base), BF16),
-            pltpu.VMEM((modes, kmax // LANES, rows, LANES), F32),
-            pltpu.VMEM((modes, kmax // LANES, rows, LANES), F32),
-            pltpu.VMEM((modes, 2, samples, kmax), F32),
+            pltpu.VMEM((freqs, samples, 2, base), BF16),
+            pltpu.VMEM((2, freqs, half, 2, base), BF16),
+            pltpu.VMEM((3, kmax // LANES, rows, LANES), F32),
+            pltpu.VMEM((3, kmax // LANES, rows, LANES), F32),
+            pltpu.VMEM((2, half, kmax), F32),
             pltpu.VMEM((NY - 1, 2, half, kmax), BF16),
             pltpu.VMEM((NY, 2, half, kmax), BF16),
             pltpu.VMEM((NZ, 2 * kmax // LANES, LANES), F32),
             pltpu.VMEM((group, 2 * kmax // LANES, LANES), F32),
             dma,
-            dma((modes, freqs)),
+            dma((freqs,)),
+            dma((2, freqs)),
             dma((modes, freqs)),
             dma((NY - 1,)), dma((NY,)),
             dma((NY,)), dma((NY,)),
-            dma((NZ,)), dma((NZ,)),
-            dma((group,)), dma((group,)),
+            dma, dma,
+            dma, dma,
         ],
         compiler_params=pltpu.CompilerParams(
             collective_id=0, has_side_effects=True, vmem_limit_bytes=32 << 20

time: 31.9 us -> 31.3 us (0.981)
  Pallas kernels: 31.1 us -> 30.6 us
    pallas_call x1, Pallas kernels: 27.6 us -> 27.1 us  [per_device(): pl.pallas_call(project_kernel, out_shape=(jax.ShapeDtypeStruct((NY, 2, ha...]
where the time goes in v4:
time: 31.3 us; the launch traced here: 31.2 us
  Pallas kernels  30.6 us (98%)
  between operations  0.64 us (2%)
    pallas_call x1, Pallas kernels, per_device(): pl.pallas_call(project_kernel, out_shape=(jax.ShapeDtypeStruct((NY, 2, ha...  27.1 us
    pallas_call x1, Pallas kernels, per_device(): pl.pallas_call(filter_kernel, out_shape=(jax.ShapeDtypeStruct((modes, 2,...  3.5 us

profile of v4, /device:TPU:1, one launch (start us, length us, event | category | flops | bytes accessed | tf_op | source)
XLA Modules:
  0.0 31.2 jit_solution(7236460248560924714)
XLA Ops:
  0.6 27.1 %shard_map.50 = (bf16[4,2,96,256]{3,2,1,0:T(8,128)(2,1)S(1)}, f32[2,256]{1,0:T(2,128)S(1)}, bf16[2,4,2,512,256]{4,3,2,1,0:T(8,128)(2,1)S(1)}) custom-call(s32[2]{0:T(128)} %ret_hbm.1, bf16[2,192,4,2,512]{4,3,2,1,0:T(2,128)(2,1)} %x_hbm.1, bf16[2,4,2,512,256]{4,3,2,1,0:T(8,128)(2,1)} %e_hbm.1), custom_call_target="tpu_custom_call" | custom-call | flops 1610612736 | bytes 8388608 | tf_op jit(solution)/shard_map/pallas_call | solution.py:265
  27.7 3.5 %shard_map.51 = (bf16[2,2,192,256]{3,2,1,0:T(8,128)(2,1)}, bf16[2,192,4,2,512]{4,3,2,1,0:T(2,128)(2,1)}) custom-call(bf16[4,2,96,256]{3,2,1,0:T(8,128)(2,1)S(1)} %get-tuple-element.5.g_ref, f32[2,256]{1,0:T(2,128)S(1)} %get-tuple-element.6.s_ref, bf16[2,4,2,512,256]{4,3,2,1,0:T(8,128)(2,1)S(1)} %get-tuple-element.7.eb), custom_call_target="tpu_custom_call" | custom-call | flops 1610612736 | bytes 8388608 | tf_op jit(solution)/shard_map/pallas_call | solution.py:299

commit v5 on v4

--- a/solution.py
+++ b/solution.py
@@ -10,6 +10,7 @@
 MESH = pl.DeviceIdType.MESH
 BF16, F32 = jnp.bfloat16, jnp.float32
 NX, NZ, NCORE, NY = 4, 8, 2, 4
+HUB = 1
 LANES = 128
 
 
@@ -52,21 +53,41 @@
     ret_copy = pltpu.make_async_copy(ret_hbm, ret_ref, ret_sem)
     ret_copy.start()
 
-    z_peers = [((x * NZ + lax.rem(z + d, NZ)) * NCORE + core, lax.rem(z + d, NZ)) for d in range(NZ)]
+    zs = [lax.rem(z + d, NZ) for d in range(NZ)]
     xs = [lax.rem(x + d, NX) for d in range(NX)]
     ys = [lax.rem(y + d, NY) for d in range(NY)]
-    cs = [core, 1 - core]
     far = [2, 1, 3, 0]
-    w_peers = [
-        ((xs[dx] * NZ + z) * NCORE + cs[dc], ys[dy])
-        for dx in far for dy in far for dc in (1, 0)
-        if (dx, dy, dc) != (0, 0, 0)
-    ]
+    flat = [(dx, dy) for dx in far for dy in far]
+
+    def on_z(d, c):
+        return {"ma": (x * NZ + zs[d]) * NCORE + c, "freq": y}
+
+    def on_xy(dx, dy, c):
+        return {"ma": (xs[dx] * NZ + z) * NCORE + c, "freq": ys[dy]}
+
     barrier = pltpu.get_barrier_semaphore()
-    for peer in w_peers:
-        pl.semaphore_signal(barrier, inc=1, device_id={"ma": peer[0], "freq": peer[1]}, device_id_type=MESH)
+
+    def greet(peer):
+        pl.semaphore_signal(barrier, inc=1, device_id=peer, device_id_type=MESH)
+
+    for dx, dy in flat:
+        greet(on_xy(dx, dy, 1 - core))
     for d in range(1, NZ):
-        pl.semaphore_signal(barrier, inc=1, device_id={"ma": z_peers[d][0], "freq": y}, device_id_type=MESH)
+        greet(on_z(d, 1 - core))
+    for d in range(1, NY):
+        greet(on_xy(0, d, core))
+
+    @pl.when(core == HUB)
+    def _():
+        for dx, dy in flat:
+            if dx:
+                greet(on_xy(dx, dy, core))
+        for d in range(1, NZ):
+            greet(on_z(d, core))
+
+    greeted = NX * NY + (NZ - 1) + (NY - 1)
+    is_hub = core if HUB == 1 else 1 - core
+    greeted = greeted + is_hub * ((NX - 1) * NY + NZ - 1)
 
     def rs_copy(i, part, t):
         return pltpu.make_async_remote_copy(
@@ -110,7 +131,7 @@
         e_copy(first, f).wait()
         project(0, first, f, xb[f].reshape(2 * samples, base))
     combine(0, samples, put_halves)
-    pl.semaphore_wait(barrier, len(w_peers) + NZ - 1)
+    pl.semaphore_wait(barrier, greeted)
     rs_copies[0].start()
     rs_copies[1].start()
     for f in range(freqs):
@@ -137,18 +158,23 @@
     keep = (ranks < ret_ref[y // 2]).astype(F32)
     power = keep * jnp.sum(share[0] * share[0] + share[1] * share[1], axis=0, keepdims=True)
     count = keep * half
+    spot = z * NCORE + core
     for p in range(parts):
-        a1[z, pl.ds(p, 1), :] = power[:, p * LANES : (p + 1) * LANES]
-        a1[z, pl.ds(parts + p, 1), :] = count[:, p * LANES : (p + 1) * LANES]
+        a1[spot, pl.ds(p, 1), :] = power[:, p * LANES : (p + 1) * LANES]
+        a1[spot, pl.ds(parts + p, 1), :] = count[:, p * LANES : (p + 1) * LANES]
 
     def z_copy(d):
         return pltpu.make_async_remote_copy(
-            src_ref=a1.at[z], dst_ref=a1.at[z], send_sem=z_send, recv_sem=z_recv,
-            device_id={"ma": z_peers[d][0], "freq": y}, device_id_type=MESH,
+            src_ref=a1.at[spot], dst_ref=a1.at[spot], send_sem=z_send, recv_sem=z_recv,
+            device_id=on_z(d, HUB), device_id_type=MESH,
         )
 
     for d in (4, 3, 5, 2, 6, 1, 7):
         z_copy(d).start()
+
+    @pl.when(core != HUB)
+    def _():
+        z_copy(0).start()
 
     g_ref[y] = share.astype(BF16)
 
@@ -164,25 +190,30 @@
     def settle(ref, count, sem):
         pltpu.make_async_copy(ref.at[pl.ds(0, count)], ref.at[pl.ds(0, count)], sem).wait()
 
-    settle(a1, NZ - 1, z_recv)
-    total = a1[0]
-    for i in range(1, NZ):
-        total = total + a1[i]
-
-    q = (x * NY + y) * NCORE + core
-    a2[q] = total
-
-    def w_copy(i):
-        return pltpu.make_async_remote_copy(
-            src_ref=a2.at[q], dst_ref=a2.at[q], send_sem=w_send, recv_sem=w_recv,
-            device_id={"ma": w_peers[i][0], "freq": w_peers[i][1]}, device_id_type=MESH,
-        )
-
-    for i in range(len(w_peers)):
-        w_copy(i).start()
-    settle(a2, len(w_peers), w_recv)
+    q = x * NY + y
+
+    @pl.when(core == HUB)
+    def _():
+        settle(a1, NZ * NCORE - 1, z_recv)
+        total = a1[0]
+        for i in range(1, NZ * NCORE):
+            total = total + a1[i]
+        a2[q] = total
+        for dx, dy in flat:
+            for c in (1 - HUB, HUB):
+                if (dx, dy, c) != (0, 0, HUB):
+                    pltpu.make_async_remote_copy(
+                        src_ref=a2.at[q], dst_ref=a2.at[q], send_sem=w_send, recv_sem=w_recv,
+                        device_id=on_xy(dx, dy, c), device_id_type=MESH,
+                    ).start()
+        settle(a2, NX * NY - 1, w_recv)
+
+    @pl.when(core != HUB)
+    def _():
+        settle(a2, NX * NY, w_recv)
+
     total = a2[0]
-    for i in range(1, NX * NY * NCORE):
+    for i in range(1, NX * NY):
         total = total + a2[i]
     scale = 1.0 / jnp.sqrt(total[:parts] / jnp.maximum(total[parts:], 1.0) + 1e-06)
     scale = jnp.concatenate([scale[p : p + 1, :] for p in range(parts)], axis=1)
@@ -199,8 +230,14 @@
         copy.wait_send()
     for d in range(1, NY):
         ag_copy(d).wait_send()
-    settle(a1, NZ - 1, z_send)
-    settle(a2, len(w_peers), w_send)
+    @pl.when(core == HUB)
+    def _():
+        settle(a1, NZ - 1, z_send)
+        settle(a2, NX * NY * NCORE - 1, w_send)
+
+    @pl.when(core != HUB)
+    def _():
+        settle(a1, NZ, z_send)
 
 
 def filter_kernel(g_ref, s_ref, eb, c_hbm, o_hbm, cb, of, ob, c_sem, o_sem):
@@ -254,7 +291,6 @@
     rows = 2 * samples
     half = samples // 2
     slab = samples * freqs * 2
-    group = NX * NY * NCORE
     visibilities, eigenmodes, retained = (
         pltpu.with_memory_space_constraint(a, pltpu.HBM) for a in (visibilities, eigenmodes, retained)
     )
@@ -280,8 +316,8 @@
             pltpu.VMEM((2, half, kmax), F32),
             pltpu.VMEM((NY - 1, 2, half, kmax), BF16),
             pltpu.VMEM((NY, 2, half, kmax), BF16),
-            pltpu.VMEM((NZ, 2 * kmax // LANES, LANES), F32),
-            pltpu.VMEM((group, 2 * kmax // LANES, LANES), F32),
+            pltpu.VMEM((NZ * NCORE, 2 * kmax // LANES, LANES), F32),
+            pltpu.VMEM((NX * NY * NCORE, 2 * kmax // LANES, LANES), F32),
             dma,
             dma((freqs,)),
             dma((2, freqs)),

time: 31.3 us -> 30.6 us (0.978)
  Pallas kernels: 30.6 us -> 29.9 us
    pallas_call x1, Pallas kernels: 27.1 us -> 26.4 us  [per_device(): pl.pallas_call(project_kernel, out_shape=(jax.ShapeDtypeStruct((NY, 2, ha...]
where the time goes in v5:
time: 30.6 us; the launch traced here: 30.5 us
  Pallas kernels  29.9 us (98%)
  between operations  0.64 us (2%)
    pallas_call x1, Pallas kernels, per_device(): pl.pallas_call(project_kernel, out_shape=(jax.ShapeDtypeStruct((NY, 2, ha...  26.4 us
    pallas_call x1, Pallas kernels, per_device(): pl.pallas_call(filter_kernel, out_shape=(jax.ShapeDtypeStruct((modes, 2,...  3.48 us

profile of v5, /device:TPU:1, one launch (start us, length us, event | category | flops | bytes accessed | tf_op | source)
XLA Modules:
  0.0 30.5 jit_solution(16301858387510513352)
XLA Ops:
  0.6 26.4 %shard_map.50 = (bf16[4,2,96,256]{3,2,1,0:T(8,128)(2,1)S(1)}, f32[2,256]{1,0:T(2,128)S(1)}, bf16[2,4,2,512,256]{4,3,2,1,0:T(8,128)(2,1)S(1)}) custom-call(s32[2]{0:T(128)} %ret_hbm.1, bf16[2,192,4,2,512]{4,3,2,1,0:T(2,128)(2,1)} %x_hbm.1, bf16[2,4,2,512,256]{4,3,2,1,0:T(8,128)(2,1)} %e_hbm.1), custom_call_target="tpu_custom_call" | custom-call | flops 1610612736 | bytes 8388608 | tf_op jit(solution)/shard_map/pallas_call | solution.py:301
  27.0 3.5 %shard_map.51 = (bf16[2,2,192,256]{3,2,1,0:T(8,128)(2,1)}, bf16[2,192,4,2,512]{4,3,2,1,0:T(2,128)(2,1)}) custom-call(bf16[4,2,96,256]{3,2,1,0:T(8,128)(2,1)S(1)} %get-tuple-element.5.g_ref, f32[2,256]{1,0:T(2,128)S(1)} %get-tuple-element.6.s_ref, bf16[2,4,2,512,256]{4,3,2,1,0:T(8,128)(2,1)S(1)} %get-tuple-element.7.eb), custom_call_target="tpu_custom_call" | custom-call | flops 1610612736 | bytes 8388608 | tf_op jit(solution)/shard_map/pallas_call | solution.py:335

commit v6 on v5

--- a/solution.py
+++ b/solution.py
@@ -12,6 +12,12 @@
 NX, NZ, NCORE, NY = 4, 8, 2, 4
 HUB = 1
 LANES = 128
+
+
+def added(terms):
+    while len(terms) > 1:
+        terms = [a + b for a, b in zip(terms[::2], terms[1::2])]
+    return terms[0]
 
 
 def project_kernel(
@@ -145,8 +151,7 @@
         project(2, second, f, xh[1, f].reshape(samples, base))
     combine(2, half, put_own)
     share = pf[...]
-    for d in range(1, NY):
-        src = ys[d]
+    for d, src in ((1, 2 * first + mine), (2, 2 * first + 1 - mine), (3, 2 * second + 1 - mine)):
         pltpu.make_async_remote_copy(
             src_ref=sbuf.at[0], dst_ref=rbuf.at[src],
             send_sem=rs_send.at[d - 1], recv_sem=rs_recv.at[src],
@@ -195,9 +200,7 @@
     @pl.when(core == HUB)
     def _():
         settle(a1, NZ * NCORE - 1, z_recv)
-        total = a1[0]
-        for i in range(1, NZ * NCORE):
-            total = total + a1[i]
+        total = added([a1[i] for i in range(NZ * NCORE)])
         a2[q] = total
         for dx, dy in flat:
             for c in (1 - HUB, HUB):
@@ -212,9 +215,7 @@
     def _():
         settle(a2, NX * NY, w_recv)
 
-    total = a2[0]
-    for i in range(1, NX * NY):
-        total = total + a2[i]
+    total = added([a2[i] for i in range(NX * NY)])
     scale = 1.0 / jnp.sqrt(total[:parts] / jnp.maximum(total[parts:], 1.0) + 1e-06)
     scale = jnp.concatenate([scale[p : p + 1, :] for p in range(parts)], axis=1)
     for m in range(modes):

time: 30.6 us -> 30.5 us (level)
  no operation moved by 1% of the time
where the time goes in v6:
time: 30.5 us
  Pallas kernels  29.8 us (98%)
  between operations  0.64 us (2%)
    pallas_call x1, Pallas kernels, per_device(): pl.pallas_call(project_kernel, out_shape=(jax.ShapeDtypeStruct((NY, 2, ha...  26.3 us
    pallas_call x1, Pallas kernels, per_device(): pl.pallas_call(filter_kernel, out_shape=(jax.ShapeDtypeStruct((modes, 2,...  3.49 us

profile of v6, /device:TPU:1, one launch (start us, length us, event | category | flops | bytes accessed | tf_op | source)
XLA Modules:
  0.0 30.5 jit_solution(2690043846967029755)
XLA Ops:
  0.6 26.3 %shard_map.50 = (bf16[4,2,96,256]{3,2,1,0:T(8,128)(2,1)S(1)}, f32[2,256]{1,0:T(2,128)S(1)}, bf16[2,4,2,512,256]{4,3,2,1,0:T(8,128)(2,1)S(1)}) custom-call(s32[2]{0:T(128)} %ret_hbm.1, bf16[2,192,4,2,512]{4,3,2,1,0:T(2,128)(2,1)} %x_hbm.1, bf16[2,4,2,512,256]{4,3,2,1,0:T(8,128)(2,1)} %e_hbm.1), custom_call_target="tpu_custom_call" | custom-call | flops 1610612736 | bytes 8388608 | tf_op jit(solution)/shard_map/pallas_call | solution.py:302
  27.0 3.5 %shard_map.51 = (bf16[2,2,192,256]{3,2,1,0:T(8,128)(2,1)}, bf16[2,192,4,2,512]{4,3,2,1,0:T(2,128)(2,1)}) custom-call(bf16[4,2,96,256]{3,2,1,0:T(8,128)(2,1)S(1)} %get-tuple-element.5.g_ref, f32[2,256]{1,0:T(2,128)S(1)} %get-tuple-element.6.s_ref, bf16[2,4,2,512,256]{4,3,2,1,0:T(8,128)(2,1)S(1)} %get-tuple-element.7.eb), custom_call_target="tpu_custom_call" | custom-call | flops 1610612736 | bytes 8388608 | tf_op jit(solution)/shard_map/pallas_call | solution.py:336
